TPU v7x, 256 devices: a whole 4x4x8 slice. The times are simulated.
256 devices in a mesh: items: 4 (over x), users: 64 (over z, y, core).
Axes of the slice: x: 4, y: 4, z: 8, core: 2. Of those that a mesh axis runs over, the one named last changes fastest.
Arguments:
- capsules: bfloat16 [4096, 8, 128], P('users'), may hold values from -6 to 6
- bank: bfloat16 [262144, 128], P(('items', 'users')), may hold values from -0.5 to 0.5
Outputs:
- relative: float32 [4096, 256], P('users', 'items')
- peak: float32 [4096], P('users')
All inputs are finite; a program needn't handle non-finite values.
Results may differ from a plain program's by a relative error of at most 0.0003.
Values may be sent and summed in bfloat16 or wider, within the bound.
A program may use at most 64 MiB of HBM per device.

v0:
```python
import jax
import jax.numpy as jnp
from jax import lax
from jax.sharding import PartitionSpec as P

BLOCK = 1024


def sent_to_all(value, axis):
    length = lax.axis_size(axis)
    return lax.all_to_all(
        jnp.broadcast_to(value[None], (length, *value.shape)), axis, 0, 0, tiled=True
    )


def of_everyone(value, axis):
    return sent_to_all(value, axis).max(axis=0)


def block_peaks(caps, rows):
    users_here = caps.shape[0]
    flat = caps.reshape(users_here * caps.shape[1], caps.shape[2])
    count = rows.shape[0] // BLOCK
    blocks = rows.reshape(count, BLOCK, rows.shape[1])

    def one_block(item_rows):
        score = lax.dot_general(
            flat, item_rows, (((1,), (1,)), ((), ())), preferred_element_type=jnp.float32
        )
        return jnp.max(score.reshape(users_here, -1), axis=1)

    return lax.map(one_block, blocks).T


def per_device(capsules, bank):
    everyone = lax.all_gather(capsules, "users", axis=0, tiled=True)
    own_block = block_peaks(everyone, bank)
    table = lax.all_to_all(own_block, "users", split_axis=0, concat_axis=1, tiled=True)
    peak = of_everyone(jnp.max(table, axis=1), "items")
    return (table - peak[:, None], peak)


def solution(mesh):
    return jax.shard_map(
        per_device,
        mesh=mesh,
        in_specs=(P("users", None, None), P(("items", "users"), None)),
        out_specs=(P("users", "items"), P("users")),
        check_vma=False,
    )
```

profile of v0, /device:TPU:1, one launch (start us, length us, event | category | flops | bytes accessed | tf_op | source)
XLA Modules:
  0.0 152.0 jit_solution(13896020500113062206)
XLA Ops:
  7.2 0.0 copy-start
  7.2 0.0 all-gather.2.cloned.1.call-start
  7.2 0.7 all-gather.2.cloned.1.call-update
  7.9 90.1 %all-gather.2.cloned.1.call-done = bf16[4096,8,128]{2,1,0:T(8,128)(2,1)} async-done(((bf16[64,8,128]{2,1,0:T(8,128)(2,1)}), bf16[4096,8,128]{2,1,0:T(8,128)(2,1)}) %all-gather.2.cloned.1.call-update) | async-done | bytes 8388624 | tf_op jit(solution)/shard_map/all_gather | solution.py:36
  98.0 0.0 copy-done
  98.0 21.6 %convolution_reduce_fusion = f32[32768]{0:T(1024)S(1)} fusion(bf16[1024,128]{1,0:T(8,128)(2,1)S(1)} %copy-done, bf16[4096,8,128]{2,1,0:T(8,128)(2,1)} %all-gather.2.cloned.1.call-done), kind=kOutput, calls=%fused_computation | convolution fusion | flops 8623456256 | bytes 8781824 | tf_op jit(solution)/shard_map/while/body/eval_jaxpr/dot_general | solution.py:27
  119.6 1.1 reduce_max.36
  120.7 0.6 reduce_max.37
  121.3 0.1 all_to_all.18
  121.4 15.0 %all_to_all.25 = f32[64,64,1]{1,2,0:T(1,128)S(1)} all-to-all(f32[64,64,1]{1,2,0:T(1,128)S(1)} %bitcast.10), channel_id=1, replica_groups=mesh['items'=4,'users'=64] {'users'}, dimensions={0} | all-to-all | bytes 32768 | tf_op jit(solution)/shard_map/all_to_all | solution.py:38
  136.4 0.1 reduce_max.38
  136.5 7.9 %all_to_all.26 = f32[4,1,64]{2,1,0:T(1,128)S(1)} all-to-all(f32[4,1,64]{2,1,0:T(1,128)S(1)} %broadcast_in_dim.5), channel_id=1, replica_groups=mesh['items'=4,'users'=64] {'items'}, dimensions={0} | all-to-all | bytes 2048 | tf_op jit(solution)/shard_map/all_to_all | solution.py:11
  144.4 0.0 copy-start.1
  144.4 0.7 copy.11
  145.1 0.0 copy-done.1
  (3 shorter events, 0.0 us)
Async XLA Ops:
  7.2 90.8 %copy-start = (bf16[1024,128]{1,0:T(8,128)(2,1)S(1)}, bf16[1024,128]{1,0:T(8,128)(2,1)}, u32[]{:S(2)}) copy-start(bf16[1024,128]{1,0:T(8,128)(2,1)} %param.3) | copy-start | bytes 786436
  7.2 90.8 %all-gather.2.cloned.1.call-start = ((), (), s32[]{:S(2)}) async-start(), calls=%async_computation.2 | async-start | bytes 8519680 | tf_op jit(solution)/shard_map/all_gather | solution.py:36
  144.4 0.7 copy-start.1
Sparse Core Ops, SparseCore 0:
  10.8 87.1 all-gather.1
where the time goes:
time: 152 us
  waiting for transfers between devices  90.8 us (60%)
  blocking collectives  22.9 us (15%)
  matrix products  21.6 us (14%)
  between operations  14.1 us (9%)
  local copies, waits for them, and re-layouts  1.92 us (1%)
    all_gather x1, waiting for transfers between devices, per_device(): everyone = lax.all_gather(capsules, 'users', axis=0, tiled=True)  90.1 us
    dot_general x1, matrix products, one_block(): lax.dot_general(flat, item_rows, (((1,), (1,)), ((), ())), preferred_elem...  21.6 us
    all_to_all x1, blocking collectives, per_device(): lax.all_to_all(own_block, 'users', split_axis=0, concat_axis=1, tiled=True)  15 us
    all_to_all x1, blocking collectives, sent_to_all(): lax.all_to_all(jnp.broadcast_to(value[None], (length, *value.shape)), axi...  7.9 us
  transfers between devices with their start and end apart: 1, of which 1 were waited for; matrix products, arithmetic and copies ran while one was open for 0% of the time, Pallas kernels for 0%

commit v1 on v0

--- a/solution.py
+++ b/solution.py
@@ -35,7 +35,9 @@
 def per_device(capsules, bank):
     everyone = lax.all_gather(capsules, "users", axis=0, tiled=True)
     own_block = block_peaks(everyone, bank)
-    table = lax.all_to_all(own_block, "users", split_axis=0, concat_axis=1, tiled=True)
+    shards = jnp.split(own_block, lax.axis_size("users"), axis=0)
+    received = lax.all_to_all(jnp.stack(shards), "users", 0, 0)
+    table = jnp.concatenate(received, axis=1)
     peak = of_everyone(jnp.max(table, axis=1), "items")
     return (table - peak[:, None], peak)
 

time: 152 us -> 155 us (1.020)
  local copies, waits for them, and re-layouts: 1.92 us -> 4.61 us
    unnamed x5 -> x68, local copies, waits for them, and re-layouts: 0.71 us -> 3.4 us
where the time goes in v1:
time: 155 us
  waiting for transfers between devices  90.8 us (59%)
  blocking collectives  22.9 us (15%)
  matrix products  21.6 us (14%)
  between operations  14.1 us (9%)
  local copies, waits for them, and re-layouts  4.61 us (3%)
    all_gather x1, waiting for transfers between devices, per_device(): everyone = lax.all_gather(capsules, 'users', axis=0, tiled=True)  90.1 us
    dot_general x1, matrix products, one_block(): lax.dot_general(flat, item_rows, (((1,), (1,)), ((), ())), preferred_elem...  21.6 us
    all_to_all x1, blocking collectives, per_device(): received = lax.all_to_all(jnp.stack(shards), 'users', 0, 0)  15 us
    all_to_all x1, blocking collectives, sent_to_all(): lax.all_to_all(jnp.broadcast_to(value[None], (length, *value.shape)), axi...  7.9 us
    unnamed x68, local copies, waits for them, and re-layouts  3.4 us
  transfers between devices with their start and end apart: 1, of which 1 were waited for; matrix products, arithmetic and copies ran while one was open for 0% of the time, Pallas kernels for 0%

profile of v1, /device:TPU:1, one launch (start us, length us, event | category | flops | bytes accessed | tf_op | source)
XLA Modules:
  0.0 154.7 jit_solution(17348725484174725983)
XLA Ops:
  7.2 0.0 copy-start
  7.2 0.0 all-gather.2.cloned.1.call-start
  7.2 0.7 all-gather.2.cloned.1.call-update
  7.9 90.1 %all-gather.2.cloned.1.call-done = bf16[4096,8,128]{2,1,0:T(8,128)(2,1)} async-done(((bf16[64,8,128]{2,1,0:T(8,128)(2,1)}), bf16[4096,8,128]{2,1,0:T(8,128)(2,1)}) %all-gather.2.cloned.1.call-update) | async-done | bytes 8388624 | tf_op jit(solution)/shard_map/all_gather | solution.py:36
  98.0 0.0 copy-done
  98.0 21.6 %convolution_reduce_fusion = f32[32768]{0:T(1024)S(1)} fusion(bf16[1024,128]{1,0:T(8,128)(2,1)S(1)} %copy-done, bf16[4096,8,128]{2,1,0:T(8,128)(2,1)} %all-gather.2.cloned.1.call-done), kind=kOutput, calls=%fused_computation | convolution fusion | flops 8623456256 | bytes 8781824 | tf_op jit(solution)/shard_map/while/body/eval_jaxpr/dot_general | solution.py:27
  119.6 1.1 reduce_max.36
  120.7 0.6 reduce_max.37
  121.4 0.1 constant_dynamic-update-slice_fusion.62
  121.4 0.1 constant_dynamic-update-slice_fusion.60
  121.5 0.1 constant_dynamic-update-slice_fusion.58
  121.6 0.1 constant_dynamic-update-slice_fusion.56
  121.7 0.1 constant_dynamic-update-slice_fusion.54
  121.8 0.1 constant_dynamic-update-slice_fusion.52
  121.9 0.1 constant_dynamic-update-slice_fusion.50
  122.0 0.1 constant_dynamic-update-slice_fusion.48
  122.1 0.1 constant_dynamic-update-slice_fusion.46
  122.1 0.1 constant_dynamic-update-slice_fusion.44
  122.2 0.1 constant_dynamic-update-slice_fusion.42
  122.3 0.1 constant_dynamic-update-slice_fusion.40
  122.4 0.1 constant_dynamic-update-slice_fusion.38
  122.5 0.1 constant_dynamic-update-slice_fusion.36
  122.6 0.1 constant_dynamic-update-slice_fusion.34
  122.7 0.1 constant_dynamic-update-slice_fusion.32
  122.8 0.1 constant_dynamic-update-slice_fusion.30
  122.8 0.1 constant_dynamic-update-slice_fusion.28
  122.9 0.1 constant_dynamic-update-slice_fusion.26
  123.0 0.1 constant_dynamic-update-slice_fusion.24
  123.1 0.1 constant_dynamic-update-slice_fusion.22
  123.2 0.1 constant_dynamic-update-slice_fusion.20
  123.3 0.1 constant_dynamic-update-slice_fusion.18
  123.4 0.1 constant_dynamic-update-slice_fusion.16
  123.5 0.1 constant_dynamic-update-slice_fusion.14
  123.5 0.1 constant_dynamic-update-slice_fusion.12
  123.6 0.1 constant_dynamic-update-slice_fusion.10
  123.7 0.1 constant_dynamic-update-slice_fusion.8
  123.8 0.1 constant_dynamic-update-slice_fusion.6
  123.9 0.1 constant_dynamic-update-slice_fusion.4
  124.0 0.1 constant_dynamic-update-slice_fusion.2
  124.1 0.1 constant_dynamic-update-slice_fusion
  124.1 15.0 %all_to_all.11 = f32[64,64,1]{1,2,0:T(1,128)S(1)} all-to-all(f32[64,64,1]{1,2,0:T(1,128)S(1)} %constant_dynamic-update-slice_fusion), channel_id=1, replica_groups=mesh['items'=4,'users'=64] {'users'}, dimensions={0} | all-to-all | bytes 32768 | tf_op jit(solution)/shard_map/all_to_all | solution.py:39
  139.1 0.1 reduce_max.38
  139.2 7.9 %all_to_all.12 = f32[4,1,64]{2,1,0:T(1,128)S(1)} all-to-all(f32[4,1,64]{2,1,0:T(1,128)S(1)} %broadcast_in_dim.5), channel_id=1, replica_groups=mesh['items'=4,'users'=64] {'items'}, dimensions={0} | all-to-all | bytes 2048 | tf_op jit(solution)/shard_map/all_to_all | solution.py:11
  147.1 0.0 copy-start.1
  147.1 0.7 copy.9
  147.8 0.0 copy-done.1
  (35 shorter events, 0.3 us)
Async XLA Ops:
  7.2 90.8 %copy-start = (bf16[1024,128]{1,0:T(8,128)(2,1)S(1)}, bf16[1024,128]{1,0:T(8,128)(2,1)}, u32[]{:S(2)}) copy-start(bf16[1024,128]{1,0:T(8,128)(2,1)} %param.3) | copy-start | bytes 786436
  7.2 90.8 %all-gather.2.cloned.1.call-start = ((), (), s32[]{:S(2)}) async-start(), calls=%async_computation.2 | async-start | bytes 8519680 | tf_op jit(solution)/shard_map/all_gather | solution.py:36
  147.1 0.7 copy-start.1
Sparse Core Ops, SparseCore 0:
  10.8 87.1 all-gather.1

commit v2 on v0

--- a/solution.py
+++ b/solution.py
@@ -33,7 +33,10 @@
 
 
 def per_device(capsules, bank):
-    everyone = lax.all_gather(capsules, "users", axis=0, tiled=True)
+    size = lax.axis_size("users")
+    parts = jnp.stack([capsules for _ in range(size)])
+    parts = lax.all_to_all(parts, "users", split_axis=0, concat_axis=0)
+    everyone = jnp.concatenate(parts, axis=0)
     own_block = block_peaks(everyone, bank)
     table = lax.all_to_all(own_block, "users", split_axis=0, concat_axis=1, tiled=True)
     peak = of_everyone(jnp.max(table, axis=1), "items")

time: 152 us -> 246 us (1.62)
  blocking collectives: 22.9 us -> 222 us
  waiting for transfers between devices: 90.8 us -> 0 us
  between operations: 14.1 us -> 0.68 us
  matrix products: 21.6 us -> 18.2 us
  local copies, waits for them, and re-layouts: 1.92 us -> 4.87 us
    all_to_all x0 -> x1, blocking collectives: none -> 197 us  [per_device(): parts = lax.all_to_all(parts, 'users', split_axis=0, concat_axis=0)]
    all_gather x1 -> x0, waiting for transfers between devices: 90.1 us -> none  [per_device(): everyone = lax.all_gather(capsules, 'users', axis=0, tiled=True)]
    dot_general x1, matrix products: 21.6 us -> 18.2 us  [one_block(): lax.dot_general(flat, item_rows, (((1,), (1,)), ((), ())), preferred_elem...]
    another operation x0 -> x1, local copies, waits for them, and re-layouts: none -> 2.96 us  [per_device(): parts = jnp.stack([capsules for _ in range(size)])]
  transfers between devices with their start and end apart: 1 -> 0, of which waited for: 1 -> 0; matrix products, arithmetic and copies ran while one was open for 0% -> 0% of each run, Pallas kernels for 0% -> 0%
where the time goes in v2:
time: 246 us
  blocking collectives  222 us (90%)
  matrix products  18.2 us (7%)
  local copies, waits for them, and re-layouts  4.87 us (2%)
    all_to_all x1, blocking collectives, per_device(): parts = lax.all_to_all(parts, 'users', split_axis=0, concat_axis=0)  197 us
    dot_general x1, matrix products, one_block(): lax.dot_general(flat, item_rows, (((1,), (1,)), ((), ())), preferred_elem...  18.2 us
    all_to_all x1, blocking collectives, per_device(): lax.all_to_all(own_block, 'users', split_axis=0, concat_axis=1, tiled=True)  16.2 us
    all_to_all x1, blocking collectives, sent_to_all(): lax.all_to_all(jnp.broadcast_to(value[None], (length, *value.shape)), axi...  7.94 us

profile of v2, /device:TPU:1, one launch (start us, length us, event | category | flops | bytes accessed | tf_op | source)
XLA Modules:
  0.0 246.1 jit_solution(8156816575158829962)
XLA Ops:
  0.6 0.0 copy-start
  0.6 3.0 %stack.2 = bf16[64,64,8,128]{3,2,1,0:T(8,128)(2,1)S(1)} broadcast(bf16[64,8,128]{2,1,0:T(8,128)(2,1)} %param.2), dimensions={1,2,3} | broadcast | bytes 8519680 | tf_op jit(solution)/shard_map/stack | solution.py:37
  3.6 197.5 %all_to_all.30 = bf16[64,64,8,128]{3,2,1,0:T(8,128)(2,1)S(1)} all-to-all(bf16[64,64,8,128]{3,2,1,0:T(8,128)(2,1)S(1)} %stack.2), channel_id=1, replica_groups=mesh['items'=4,'users'=64] {'users'}, dimensions={0} | all-to-all | bytes 16777216 | tf_op jit(solution)/shard_map/all_to_all | solution.py:38
  201.1 0.0 copy-done
  201.1 18.2 %convolution_reduce_fusion = f32[32768]{0:T(1024)S(1)} fusion(bf16[32768,128]{1,0:T(8,128)(2,1)S(1)} %bitcast.8, bf16[1024,128]{1,0:T(8,128)(2,1)S(1)} %copy-done), kind=kOutput, calls=%fused_computation | convolution fusion | flops 8623456256 | bytes 8781824 | tf_op jit(solution)/shard_map/while/body/eval_jaxpr/dot_general | solution.py:27
  219.3 1.1 reduce_max.36
  220.5 0.6 reduce_max.37
  221.1 0.1 all_to_all.22
  221.2 16.2 %all_to_all.31 = f32[64,64,1]{1,2,0:T(1,128)S(1)} all-to-all(f32[64,64,1]{1,2,0:T(1,128)S(1)} %bitcast.10), channel_id=1, replica_groups=mesh['items'=4,'users'=64] {'users'}, dimensions={0} | all-to-all | bytes 32768 | tf_op jit(solution)/shard_map/all_to_all | solution.py:41
  237.3 0.1 reduce_max.38
  237.4 7.9 %all_to_all.32 = f32[4,1,64]{2,1,0:T(1,128)S(1)} all-to-all(f32[4,1,64]{2,1,0:T(1,128)S(1)} %broadcast_in_dim.5), channel_id=1, replica_groups=mesh['items'=4,'users'=64] {'items'}, dimensions={0} | all-to-all | bytes 2048 | tf_op jit(solution)/shard_map/all_to_all | solution.py:11
  245.4 0.0 copy-start.1
  245.4 0.7 copy.11
  246.1 0.0 copy-done.1
  (3 shorter events, 0.0 us)
Async XLA Ops:
  0.6 200.5 %copy-start = (bf16[1024,128]{1,0:T(8,128)(2,1)S(1)}, bf16[1024,128]{1,0:T(8,128)(2,1)}, u32[]{:S(2)}) copy-start(bf16[1024,128]{1,0:T(8,128)(2,1)} %param.3) | copy-start | bytes 786436
  245.4 0.7 copy-start.1
